TPU v7x, 512 devices: a whole 4x4x16 slice. The times are simulated.
512 devices in a mesh: row: 16 (over z_lo, x), col: 32 (over y, z_hi, core).
Axes of the slice: x: 4, y: 4, z: 16 (z_hi: 4, z_lo: 4; z = z_hi * 4 + z_lo), core: 2. Of those that a mesh axis runs over, the one named last changes fastest.
Arguments:
- potential_temp: bfloat16 [64, 1024, 1024], P(None, 'col', 'row'), may hold values from -6 to 6
- humidity: bfloat16 [64, 1024, 1024], P(None, 'col', 'row'), may hold values from 0.099609375 to 1
- absorb: float32 [4, 64], replicated, may hold values from 0.002 to 0.2
- solar_flux: float32 [4], replicated, may hold values from 2 to 8
- emission: float32 [4], replicated, may hold values from 0.5 to 4
- sunlit: int32 [16, 32], replicated, may hold values from 0 to 2048
- project: float32 [32, 64], replicated, may hold values from -0.75 to 0.75
- restore: float32 [64, 32], replicated, may hold values from -1 to 1
- east_basis: bfloat16 [1024, 1024], replicated, may hold values from -0.1875 to 0.1875
- north_basis: bfloat16 [1024, 1024], replicated, may hold values from -0.1875 to 0.1875
- east_weight: float32 [1024], replicated, may hold values from 0.5 to 2
- north_weight: float32 [1024], replicated, may hold values from 0.5 to 2
- east_eigen: float32 [1024], replicated, may hold values from 0.05 to 4
- north_eigen: float32 [1024], replicated, may hold values from 0.05 to 4
- coupling: float32 [32], replicated, may hold values from 0.05 to 2
Outputs:
- new_state: bfloat16 [64, 1024, 1024], P(None, 'col', 'row')
All inputs are finite; a program needn't handle non-finite values.
Results may differ from a plain program's by a relative error of at most 0.01.
Values may be sent and summed in bfloat16 or wider, within the bound.
No kernel may reach another device: no remote copies, remote signals or barrier semaphores. Data moves between devices by JAX's collectives and lax.ppermute only.
A program may use at most 64 MiB of HBM per device.

v0:
```python
import jax
import jax.numpy as jnp
from jax import lax
from jax.sharding import PartitionSpec as P


def lower_triangle(levels):
    level_index = jnp.arange(levels, dtype=jnp.int32)
    return (level_index[:, None] >= level_index[None, :]).astype(jnp.float32)


def shortwave(vapour, absorb, solar_flux, triangle):
    heating = jnp.zeros(vapour.shape, jnp.float32)
    for band_index in range(absorb.shape[0]):
        optical = absorb[band_index][:, None] * vapour
        column_depth = jnp.dot(
            triangle, optical, precision=lax.Precision.HIGHEST, preferred_element_type=jnp.float32
        )
        heating = heating + solar_flux[band_index] * (
            jnp.exp(optical - column_depth) - jnp.exp(-column_depth)
        )
    return heating


def longwave(column_temp, vapour, absorb, emission):
    cooling = jnp.zeros(vapour.shape, jnp.float32)
    for band_index in range(absorb.shape[0]):
        optical = absorb[band_index][:, None] * vapour
        cooling = cooling + emission[band_index] * (1.0 - jnp.exp(-optical)) * column_temp
    return cooling


def local(
    potential_temp,
    humidity,
    absorb,
    solar_flux,
    emission,
    sunlit,
    project,
    restore,
    east_basis,
    north_basis,
    east_weight,
    north_weight,
    east_eigen,
    north_eigen,
    coupling,
):
    levels, east_local, north_local = potential_temp.shape
    columns = east_local * north_local
    column_temp = potential_temp.reshape(levels, columns).astype(jnp.float32)
    vapour = humidity.reshape(levels, columns).astype(jnp.float32)
    triangle = lower_triangle(levels)
    row_place = lax.axis_index("row")
    col_place = lax.axis_index("col")
    lit_count = sunlit[row_place, col_place]
    position = jnp.arange(columns, dtype=jnp.int32)[None, :]
    heating = shortwave(vapour, absorb, solar_flux, triangle) * (position < lit_count).astype(
        jnp.float32
    )
    forcing = column_temp + heating - longwave(column_temp, vapour, absorb, emission)
    modes = project.shape[0]
    modal_field = jnp.dot(
        project, forcing, precision=lax.Precision.HIGHEST, preferred_element_type=jnp.float32
    ).astype(jnp.bfloat16)
    modal_field = modal_field.reshape(modes, east_local, north_local)
    east_scaled = (east_basis.astype(jnp.float32) * east_weight[:, None]).astype(jnp.bfloat16)
    north_scaled = (north_basis.astype(jnp.float32) * north_weight[:, None]).astype(jnp.bfloat16)
    spectral_east = jnp.einsum(
        "xi,mxy->miy",
        east_scaled,
        lax.all_to_all(modal_field, "col", split_axis=0, concat_axis=1, tiled=True),
        preferred_element_type=jnp.float32,
    ).astype(jnp.bfloat16)
    turned = lax.all_to_all(spectral_east, "row", split_axis=1, concat_axis=2, tiled=True)
    spectral = jnp.einsum("miy,yj->mij", turned, north_scaled, preferred_element_type=jnp.float32)
    gravity = lax.dynamic_slice_in_dim(coupling, col_place * turned.shape[0], turned.shape[0])
    east_roots = lax.dynamic_slice_in_dim(east_eigen, row_place * turned.shape[1], turned.shape[1])
    divisor = 1.0 + gravity[:, None, None] * (east_roots[:, None] + north_eigen[None, :])[None]
    scaled = (spectral / divisor).astype(jnp.bfloat16)
    solved = jnp.einsum(
        "mij,yj->miy", scaled, north_basis, preferred_element_type=jnp.float32
    ).astype(jnp.bfloat16)
    result = lax.all_to_all(
        jnp.einsum(
            "xi,miy->mxy",
            east_basis,
            lax.all_to_all(solved, "row", split_axis=2, concat_axis=1, tiled=True),
            preferred_element_type=jnp.float32,
        ).astype(jnp.bfloat16),
        "col",
        split_axis=1,
        concat_axis=0,
        tiled=True,
    )
    difference = result.reshape(modes, columns).astype(jnp.float32) - modal_field.reshape(
        modes, columns
    ).astype(jnp.float32)
    correction = jnp.dot(
        restore, difference, precision=lax.Precision.HIGHEST, preferred_element_type=jnp.float32
    )
    return (forcing + correction).astype(jnp.bfloat16).reshape(levels, east_local, north_local)


def solution(mesh):
    in_specs = (
        P(None, "col", "row"),
        P(None, "col", "row"),
        P(),
        P(),
        P(),
        P(),
        P(),
        P(),
        P(),
        P(),
        P(),
        P(),
        P(),
        P(),
        P(),
    )
    out_specs = P(None, "col", "row")
    return jax.shard_map(local, mesh=mesh, in_specs=in_specs, out_specs=out_specs, check_vma=False)
```

profile of v0, /device:TPU:1, one launch (start us, length us, event | category | flops | bytes accessed | tf_op | source)
XLA Modules:
  0.0 119.9 jit_solution(14099881757313957622)
XLA Ops:
  0.0 1.3 %dynamic_slice.9 = s32[1,1]{1,0:T(1,128)} dynamic-slice(s32[16,32]{1,0:T(8,128)} %param.20, s32[]{:T(128)S(6)} %select_n.10, s32[]{:T(128)S(6)} %select_n.11), dynamic_slice_sizes={1,1} | dynamic-slice | bytes 12 | tf_op jit(solution)/shard_map/dynamic_slice | solution.py:57
  1.3 0.6 fusion.36
  1.9 0.8 slice_bitcast_fusion
  2.8 1.5 %reshape.71 = f32[64,2048]{1,0:T(8,128)S(1)} reshape(bf16[64,32,64]{2,1,0:T(8,128)(2,1)} %param.16) | data formatting | bytes 786432 | tf_op jit(solution)/shard_map/convert_element_type | solution.py:53
  5.9 0.7 fusion.38
  6.5 0.7 fusion.39
  7.6 6.4 %multiply_subtract_fusion = f32[64,2048]{1,0:T(8,128)S(1)} fusion(f32[64,2048]{1,0:T(8,128)S(1)} %reshape.70, f32[64,2048]{1,0:T(8,128)S(1)} %fusion.17, f32[64,2048]{1,0:T(8,128)S(1)} %fusion.19, f32[64,2048]{1,0:T(8,128)S(1)} %fusion.21, f32[64,2048]{1,0:T(8,128)S(1)} %reshape.71, f32[]{:T(128)} %bitcast.12, f32[]{:T(128)} %bitcast.11, f32[]{:T(128)} %bitcast.10, ...), kind=kOutput, calls=%fused_computation.20 | convolution fusion | flops 106303488 | bytes 3154976 | tf_op jit(solution)/shard_map/dot_general | solution.py:16
  14.9 36.1 %all_to_all.48 = bf16[32,2,1024]{2,1,0:T(2,128)(2,1)S(1)} all-to-all(bf16[32,2,1024]{2,1,0:T(2,128)(2,1)S(1)} %reshape.80), channel_id=1, replica_groups=mesh['row'=16,'col'=32] {'col'}, dimensions={0} | all-to-all | bytes 262144 | tf_op jit(solution)/shard_map/all_to_all | solution.py:73
  51.3 0.6 fusion.10
  52.8 2.2 %reduce.4 = bf16[1024,64]{1,0:T(8,128)(2,1)S(1)} reduce(bf16[1024,1,64]{2,1,0:T(2,128)(2,1)S(1)} %bitcast.64, bf16[]{:T(256)} %broadcast.20), dimensions={1}, to_apply=%bitcast.47.reduce_sub_computation | reduce | bytes 262146
  55.0 0.9 reshape.82
  55.9 6.7 %all-to-all-start.1 = ((bf16[16,2,2048]{2,1,0:T(2,128)(2,1)}), bf16[16,2,2048]{2,1,0:T(2,128)(2,1)S(1)}, u32[]{:S(2)}, u32[]{:S(2)}) async-start(bf16[16,2,2048]{2,1,0:T(2,128)(2,1)} %reshape.82), calls=%async_computation.1 | async-start | bytes 262144 | tf_op jit(solution)/shard_map/all_to_all | solution.py:76
  62.6 1.3 %dynamic_slice.10 = f32[1]{0:T(128)} dynamic-slice(f32[32]{0:T(128)} %param.29, s32[]{:T(128)S(6)} %select_n.11), dynamic_slice_sizes={1} | dynamic-slice | bytes 12 | tf_op jit(solution)/shard_map/dynamic_slice | solution.py:78
  63.9 1.3 %dynamic_slice.11 = f32[64]{0:T(128)} dynamic-slice(f32[1024]{0:T(1024)} %param.27, s32[]{:T(128)S(6)} %select_n.12), dynamic_slice_sizes={64} | dynamic-slice | bytes 516 | tf_op jit(solution)/shard_map/dynamic_slice | solution.py:79
  65.2 5.4 %all-to-all-done.1 = bf16[16,2,2048]{2,1,0:T(2,128)(2,1)S(1)} async-done(((bf16[16,2,2048]{2,1,0:T(2,128)(2,1)}), bf16[16,2,2048]{2,1,0:T(2,128)(2,1)S(1)}, u32[]{:S(2)}, u32[]{:S(2)}) %all-to-all-start.1) | async-done | bytes 131104 | tf_op jit(solution)/shard_map/all_to_all | solution.py:76
  72.0 4.2 %fusion.11 = bf16[1,64,1024]{2,1,0:T(8,128)(2,1)S(1)} fusion(bf16[1024,1024]{1,0:T(8,128)(2,1)} %param.24, bf16[64,1024]{1,0:T(8,128)(2,1)S(1)} %reshape.67, f32[1024]{0:T(1024)} %param.26, f32[1024]{0:T(1024)} %param.28, f32[64]{0:T(128)} %dynamic_slice.11, f32[]{:T(128)} %bitcast.18), kind=kOutput, calls=%fused_computation.17 | convolution fusion | flops 271974400 | bytes 2367748 | tf_op jit(solution)/shard_map/mij,yj->miy/dot_general | solution.py:82
  76.5 2.2 %reduce.5 = bf16[1024,64]{1,0:T(8,128)(2,1)S(1)} reduce(bf16[1024,1,64]{2,1,0:T(2,128)(2,1)S(1)} %bitcast.66, bf16[]{:T(256)} %broadcast.20), dimensions={1}, to_apply=%bitcast.49.reduce_sub_computation | reduce | bytes 262146
  79.0 11.3 %all_to_all.49 = bf16[16,2,2048]{2,1,0:T(2,128)(2,1)S(1)} all-to-all(bf16[16,2,2048]{2,1,0:T(2,128)(2,1)S(1)} %reshape.84), channel_id=1, replica_groups=mesh['row'=16,'col'=32] {'row'}, dimensions={0} | all-to-all | bytes 262144 | tf_op jit(solution)/shard_map/all_to_all | solution.py:89
  91.7 0.8 fusion.12
  92.9 2.2 %reduce.6 = bf16[1024,64]{1,0:T(8,128)(2,1)S(1)} reduce(bf16[1024,1,64]{2,1,0:T(2,128)(2,1)S(1)} %bitcast.65, bf16[]{:T(256)} %broadcast.20), dimensions={1}, to_apply=%bitcast.51.reduce_sub_computation | reduce | bytes 262146
  95.3 20.7 %all_to_all.50 = bf16[32,2,1024]{2,1,0:T(2,128)(2,1)S(1)} all-to-all(bf16[32,2,1024]{2,1,0:T(2,128)(2,1)S(1)} %reshape.86), channel_id=1, replica_groups=mesh['row'=16,'col'=32] {'col'}, dimensions={0} | all-to-all | bytes 262144 | tf_op jit(solution)/shard_map/all_to_all | solution.py:85
  116.3 1.5 %convert_reduce_fusion = f32[1024,64]{1,0:T(8,128)S(1)} fusion(bf16[1024,1,64]{2,1,0:T(2,128)(2,1)S(1)} %reshape.87), kind=kLoop, calls=%fused_computation.19 | loop fusion | flops 65536 | bytes 393216 | tf_op jit(solution)/shard_map/convert_element_type | solution.py:97
  118.0 0.6 fusion.1
  118.6 1.3 %reshape.69 = bf16[64,32,64]{2,1,0:T(8,128)(2,1)} reshape(bf16[64,2048]{1,0:T(8,128)(2,1)S(1)} %fusion.1) | data formatting | bytes 524288 | tf_op jit(solution)/shard_map/reshape | solution.py:103
  (40 shorter events, 8.4 us)
Async XLA Ops:
  0.0 118.0 %copy-start = (f32[64,32]{0,1:T(8,128)S(1)}, f32[64,32]{0,1:T(8,128)}, u32[]{:S(2)}) copy-start(f32[64,32]{0,1:T(8,128)} %param.22) | copy-start | bytes 24580
  2.8 3.1 %copy-start.4 = (f32[4]{0:T(128)S(1)}, f32[4]{0:T(128)}, u32[]{:S(2)}) copy-start(f32[4]{0:T(128)} %param.18) | copy-start | bytes 52
  2.8 3.8 %copy-start.5 = (f32[4]{0:T(128)S(1)}, f32[4]{0:T(128)}, u32[]{:S(2)}) copy-start(f32[4]{0:T(128)} %param.19) | copy-start | bytes 52
  2.8 4.4 %copy-start.2 = (bf16[64,32,64]{2,1,0:T(8,128)(2,1)S(1)}, bf16[64,32,64]{2,1,0:T(8,128)(2,1)}, u32[]{:S(2)}) copy-start(bf16[64,32,64]{2,1,0:T(8,128)(2,1)} %param.15) | copy-start | bytes 786436
  7.6 6.4 %copy-start.3 = (f32[32,64]{1,0:T(8,128)S(1)}, f32[32,64]{1,0:T(8,128)}, u32[]{:S(2)}) copy-start(f32[32,64]{1,0:T(8,128)} %param.21) | copy-start | bytes 24580
  14.0 37.2 %copy-start.1 = (bf16[1024,1024]{1,0:T(8,128)(2,1)S(1)}, bf16[1024,1024]{1,0:T(8,128)(2,1)}, u32[]{:S(2)}) copy-start(bf16[1024,1024]{1,0:T(8,128)(2,1)} %param.23) | copy-start | bytes 6291460
  14.0 37.2 %copy-start.6 = (f32[1024]{0:T(1024)S(1)}, f32[1024]{0:T(1024)}, u32[]{:S(2)}) copy-start(f32[1024]{0:T(1024)} %param.25) | copy-start | bytes 12292
  55.9 14.6 %all-to-all-start.1 = ((bf16[16,2,2048]{2,1,0:T(2,128)(2,1)}), bf16[16,2,2048]{2,1,0:T(2,128)(2,1)S(1)}, u32[]{:S(2)}, u32[]{:S(2)}) async-start(bf16[16,2,2048]{2,1,0:T(2,128)(2,1)} %reshape.82), calls=%async_computation.1 | async-start | bytes 262144 | tf_op jit(solution)/shard_map/all_to_all | solution.py:76
where the time goes:
time: 121 us; the launch traced here: 120 us
  blocking collectives  68.1 us (56%)
  local copies, waits for them, and re-layouts  16.2 us (13%)
  matrix products  14.5 us (12%)
  other arithmetic  8.73 us (7%)
  starting transfers between devices  6.67 us (6%)
  waiting for transfers between devices  5.36 us (4%)
    all_to_all x1, blocking collectives, local(): lax.all_to_all(modal_field, 'col', split_axis=0, concat_axis=1, tiled=True)  36.1 us
    all_to_all x1, blocking collectives, local(): lax.all_to_all(jnp.einsum('xi,miy->mxy', east_basis, lax.all_to_all(solve...  20.7 us
    all_to_all x1, blocking collectives, local(): lax.all_to_all(solved, 'row', split_axis=2, concat_axis=1, tiled=True)  11.3 us
    dot_general x4, matrix products, shortwave(): jnp.dot(triangle, optical, precision=lax.Precision.HIGHEST, preferred_ele...  7.9 us
    all_to_all x1, starting transfers between devices, local(): lax.all_to_all(spectral_east, 'row', split_axis=1, concat_axis=2, tiled=T...  6.67 us
    unnamed x3, other arithmetic  6.56 us
    all_to_all x1, waiting for transfers between devices, local(): lax.all_to_all(spectral_east, 'row', split_axis=1, concat_axis=2, tiled=T...  5.36 us
    dot_general x1, matrix products, local(): jnp.einsum('mij,yj->miy', scaled, north_basis, preferred_element_type=jnp...  4.17 us
  transfers between devices with their start and end apart: 1, of which 1 were waited for; matrix products, arithmetic and copies ran while one was open for 2% of the time, Pallas kernels for 0%

commit v1 on v0

v1 whole, which is shorter than its diff:
```python
import jax
import jax.numpy as jnp
from jax import lax
from jax.experimental import pallas as pl
from jax.experimental.pallas import tpu as pltpu
from jax.sharding import PartitionSpec as P

F32 = jnp.float32
BF16 = jnp.bfloat16
HALF = 64
LANES = 128
VMEM_LIMIT = 12 * 1024 * 1024


def dot(a, b, da, db):
    return lax.dot_general(a, b, (((da,), (db,)), ((), ())), preferred_element_type=F32)


def fold(v):
    n = v.shape[0] // 2
    return jnp.concatenate([v[:n], v[n:]], axis=1)


def unfold(v):
    k, n, _ = v.shape
    return jnp.concatenate([v[:, :, :HALF], v[:, :, HALF:]], axis=1).reshape(k * 2 * n, HALF)


def halves(v):
    high = v.astype(BF16)
    return high, (v - high.astype(F32)).astype(BF16)


def left_terms(v):
    high, low = halves(v)
    return jnp.concatenate([high, low, high], axis=1)


def right_terms(v):
    high, low = halves(v)
    return jnp.concatenate([high, high, low], axis=0)


def column_of(row, first, rows, lane):
    place = lax.broadcasted_iota(jnp.int32, (rows, LANES), 0) + first
    return jnp.sum(jnp.where(lane == place, jnp.broadcast_to(row, (rows, LANES)), 0.0), axis=1, keepdims=True)


def physics(absorb, flux, emission, sunlit, temp, vapour, project, wx, wy, forcing, send, modal, scratch):
    levels = temp.shape[0]
    bands = absorb.shape[0]
    rows = temp.shape[1] // 2
    r = lax.axis_index("row")
    c = lax.axis_index("col")
    shape = (rows, LANES)
    lane = lax.broadcasted_iota(jnp.int32, shape, 1)
    upper = lane >= HALF
    number = lax.broadcasted_iota(jnp.int32, shape, 0) * HALF + lane + jnp.where(upper, rows * HALF - HALF, 0)
    lit = (number < sunlit[r, c]).astype(F32)
    through = [lit * flux[b] for b in range(bands)]
    before = through[0] + through[1] + through[2] + through[3]
    emitted = emission[0] + emission[1] + emission[2] + emission[3]
    for level in range(levels):
        t = fold(temp[level]).astype(F32)
        h = fold(vapour[level]).astype(F32)
        kept = None
        after = None
        for b in range(bands):
            pass_through = jnp.exp(h * (-absorb[b, level]))
            through[b] = through[b] * pass_through
            part = pass_through * emission[b]
            kept = part if kept is None else kept + part
            after = through[b] if after is None else after + through[b]
        forcing[level] = t + (before - after) - (emitted - kept) * t
        before = after
    left = left_terms(project[...])
    for p in range(0, rows, 2):
        field = jnp.concatenate([forcing[:, p, :], forcing[:, p + 1, :]], axis=1)
        out = dot(left, right_terms(field), 1, 0)
        scratch[:, p, :] = out[:, :LANES]
        scratch[:, p + 1, :] = out[:, LANES:]
    per_row = LANES // (2 * rows)
    x_row = wx[pl.ds(c // per_row, 1), :]
    first = (c % per_row) * (2 * rows)
    east = jnp.where(upper, column_of(x_row, first + rows, rows, lane), column_of(x_row, first, rows, lane))
    y_row = wy[pl.ds(r // 2, 1), :]
    y_row = jnp.broadcast_to(y_row, shape)
    north = jnp.where(upper == (r % 2 == 1), y_row, pltpu.roll(y_row, HALF, 1))
    weight = east * north
    field = scratch[...]
    modal[...] = field.astype(BF16)
    send[...] = (field * weight[None]).astype(BF16)


def scatter_blocks(wide, out):
    n = wide.shape[0] // 2
    for b in range(wide.shape[1] // LANES):
        top = wide[:n, b * LANES : (b + 1) * LANES]
        low = wide[n:, b * LANES : (b + 1) * LANES]
        out[2 * b] = jnp.concatenate([top[:, :HALF], low[:, :HALF]], axis=1)
        out[2 * b + 1] = jnp.concatenate([top[:, HALF:], low[:, HALF:]], axis=1)


def to_east(got, basis, out):
    wide = dot(unfold(got[...]), basis[...], 0, 0).astype(BF16)
    scatter_blocks(wide, out)


def solve(coupling, got, basis, east, north, out, scaled):
    r = lax.axis_index("row")
    c = lax.axis_index("col")
    gravity = coupling[c]
    mine = unfold(got[...])
    spectral = dot(mine, basis[...], 0, 0)
    n = spectral.shape[0]
    lane = lax.broadcasted_iota(jnp.int32, (n, LANES), 1)
    roots = column_of(east[pl.ds(r // 2, 1), :], (r % 2) * HALF, n, lane)
    for b in range(spectral.shape[1] // LANES):
        divisor = 1.0 + gravity * (roots + north[b : b + 1, :])
        scaled[:, b * LANES : (b + 1) * LANES] = (spectral[:, b * LANES : (b + 1) * LANES] / divisor).astype(BF16)
    wide = dot(scaled[...], basis[...], 1, 1).astype(BF16)
    scatter_blocks(wide, out)


def from_east(got, basis, out):
    solved = dot(basis[...], unfold(got[...]), 1, 0).astype(BF16)
    rows = 2 * out.shape[1]
    for c in range(out.shape[0]):
        out[c] = fold(solved[c * rows : (c + 1) * rows])


def finish(got, modal, forcing, restore, out, difference, total):
    difference[...] = got[...].astype(F32) - modal[...].astype(F32)
    rows = difference.shape[1]
    left = left_terms(restore[...])
    for p in range(0, rows, 2):
        field = jnp.concatenate([difference[:, p, :], difference[:, p + 1, :]], axis=1)
        correction = dot(left, right_terms(field), 1, 0)
        total[:, p, :] = forcing[:, p, :] + correction[:, :LANES]
        total[:, p + 1, :] = forcing[:, p + 1, :] + correction[:, LANES:]
    for level in range(out.shape[0]):
        v = total[level].astype(BF16)
        out[level, :rows, :] = v[:, :HALF]
        out[level, rows:, :] = v[:, HALF:]


SMEM = pl.BlockSpec(memory_space=pltpu.SMEM)
VMEM = pl.BlockSpec(memory_space=pltpu.VMEM)


def call(body, smem, vmem, outs, scratch, *operands):
    return pl.pallas_call(
        body,
        in_specs=[SMEM] * smem + [VMEM] * vmem,
        out_specs=[VMEM] * len(outs),
        out_shape=[jax.ShapeDtypeStruct(shape, dtype) for shape, dtype in outs],
        scratch_shapes=[pltpu.VMEM(shape, dtype) for shape, dtype in scratch],
        compiler_params=pltpu.CompilerParams(vmem_limit_bytes=VMEM_LIMIT),
    )(*operands)


def exchange(v, axis):
    return lax.all_to_all(v, axis, split_axis=0, concat_axis=0, tiled=True)


def local(
    potential_temp,
    humidity,
    absorb,
    solar_flux,
    emission,
    sunlit,
    project,
    restore,
    east_basis,
    north_basis,
    east_weight,
    north_weight,
    east_eigen,
    north_eigen,
    coupling,
):
    levels, east_local, north_local = potential_temp.shape
    modes = project.shape[0]
    rows = east_local // 2
    n_row = north_basis.shape[0] // north_local
    tile = (rows, LANES)
    block = (HALF // 2, LANES)
    lanes = lambda v: v.reshape(-1, LANES)
    forcing, send, modal = call(
        physics,
        4,
        5,
        [((levels, *tile), F32), ((modes, *tile), BF16), ((modes, *tile), BF16)],
        [((modes, *tile), F32)],
        absorb,
        solar_flux,
        emission,
        sunlit,
        potential_temp,
        humidity,
        project,
        lanes(east_weight),
        lanes(north_weight),
    )
    (send,) = call(to_east, 0, 2, [((n_row, *block), BF16)], [], exchange(send, "col"), east_basis)
    (send,) = call(
        solve,
        1,
        4,
        [((n_row, *block), BF16)],
        [((HALF, north_basis.shape[0]), BF16)],
        coupling,
        exchange(send, "row"),
        north_basis,
        lanes(east_eigen),
        lanes(north_eigen),
    )
    (send,) = call(from_east, 0, 2, [((modes, *tile), BF16)], [], exchange(send, "row"), east_basis)
    (out,) = call(
        finish,
        0,
        4,
        [((levels, east_local, north_local), BF16)],
        [((modes, *tile), F32), ((levels, *tile), F32)],
        exchange(send, "col"),
        modal,
        forcing,
        restore,
    )
    return out


def solution(mesh):
    spread = P(None, "col", "row")
    in_specs = (spread, spread) + (P(),) * 13
    return jax.shard_map(local, mesh=mesh, in_specs=in_specs, out_specs=spread, check_vma=False)
```

time: 121 us -> 102 us (0.84)
  matrix products: 14.5 us -> 0 us
  waiting for transfers between devices: 5.36 us -> 15.6 us
  other arithmetic: 8.73 us -> 0 us
  Pallas kernels: 0 us -> 7.75 us
  blocking collectives: 68.1 us -> 61.7 us
  local copies, waits for them, and re-layouts: 16.2 us -> 10.1 us
    dot_general x9 -> x0, matrix products: 14.5 us -> none  [the longest x4 7.9 us: shortwave(): jnp.dot(triangle, optical, precision=lax.Precision.HIGHEST, preferred_ele...]
    all_to_all x1, waiting for transfers between devices: 5.36 us -> 15.6 us  [exchange(): return lax.all_to_all(v, axis, split_axis=0, concat_axis=0, tiled=True)]
    pallas_call x0 -> x5, Pallas kernels: none -> 7.75 us  [call(): pl.pallas_call(body, in_specs=[SMEM] * smem + [VMEM] * vmem, out_specs=[V...]
    unnamed x23 -> x33, local copies, waits for them, and re-layouts: 3.21 us -> 10.1 us
    unnamed x3 -> x0, other arithmetic: 6.56 us -> none
    all_to_all x3, blocking collectives: 68.1 us -> 61.7 us  [exchange(): return lax.all_to_all(v, axis, split_axis=0, concat_axis=0, tiled=True)]
    dynamic_slice x3 -> x0, local copies, waits for them, and re-layouts: 3.88 us -> none  [the longest x1 1.31 us: local(): lax.dynamic_slice_in_dim(coupling, col_place * turned.shape[0], turned.sh...]
    convert_element_type x6 -> x0, local copies, waits for them, and re-layouts: 3.28 us -> none  [the longest x1 1.52 us: local(): vapour = humidity.reshape(levels, columns).astype(jnp.float32)]
  transfers between devices with their start and end apart: 1 -> 1, of which waited for: 1 -> 1; matrix products, arithmetic and copies ran while one was open for 2% -> 0% of each run, Pallas kernels for 0% -> 0%
where the time goes in v1:
time: 102 us; the launch traced here: 101 us
  blocking collectives  61.7 us (60%)
  waiting for transfers between devices  15.6 us (15%)
  local copies, waits for them, and re-layouts  10.1 us (10%)
  Pallas kernels  7.75 us (8%)
  starting transfers between devices  5.8 us (6%)
    all_to_all x3, blocking collectives, exchange(): return lax.all_to_all(v, axis, split_axis=0, concat_axis=0, tiled=True)  61.7 us
    all_to_all x1, waiting for transfers between devices, exchange(): return lax.all_to_all(v, axis, split_axis=0, concat_axis=0, tiled=True)  15.6 us
    unnamed x33, local copies, waits for them, and re-layouts  10.1 us
    pallas_call x5, Pallas kernels, call(): pl.pallas_call(body, in_specs=[SMEM] * smem + [VMEM] * vmem, out_specs=[V...  7.75 us
    all_to_all x1, starting transfers between devices, exchange(): return lax.all_to_all(v, axis, split_axis=0, concat_axis=0, tiled=True)  5.8 us
  transfers between devices with their start and end apart: 1, of which 1 were waited for; matrix products, arithmetic and copies ran while one was open for 0% of the time, Pallas kernels for 0%

profile of v1, /device:TPU:1, one launch (start us, length us, event | category | flops | bytes accessed | tf_op | source)
XLA Modules:
  0.0 101.1 jit_solution(122085281335569203)
XLA Ops:
  0.0 1.1 %copy-done.3 = bf16[64,32,64]{2,1,0:T(8,128)(2,1)S(1)} copy-done((bf16[64,32,64]{2,1,0:T(8,128)(2,1)S(1)}, bf16[64,32,64]{2,1,0:T(8,128)(2,1)}, u32[]{:S(2)}) %copy-start.3) | copy-done | bytes 262168
  1.1 1.0 %copy-done.4 = bf16[64,32,64]{2,1,0:T(8,128)(2,1)S(1)} copy-done((bf16[64,32,64]{2,1,0:T(8,128)(2,1)S(1)}, bf16[64,32,64]{2,1,0:T(8,128)(2,1)}, u32[]{:S(2)}) %copy-start.4) | copy-done | bytes 262168
  2.1 0.7 copy-done.5
  2.8 0.7 copy-done.6
  3.5 0.7 copy-done.7
  4.2 0.7 copy-done.8
  4.9 0.7 copy-done.11
  5.6 0.7 copy-done.12
  6.2 0.7 copy-done.13
  6.9 2.0 %shard_map.145 = (f32[64,16,128]{2,1,0:T(8,128)S(1)}, bf16[32,16,128]{2,1,0:T(8,128)(2,1)S(1)}, bf16[32,16,128]{2,1,0:T(8,128)(2,1)S(1)}) custom-call(f32[4,64]{1,0:T(4,128)S(1)} %copy-done.11, f32[4]{0:T(128)S(1)} %copy-done.12, f32[4]{0:T(128)S(1)} %copy-done.13, s32[16,32]{1,0:T(8,128)S(1)} %copy-done.6, bf16[64,32,64]{2,1,0:T(8,128)(2,1)S(1)} %copy-done.3, ...), custom_call_target="tpu_custom_call" | custom-call | tf_op jit(solution)/shard_map/pallas_call | solution.py:152
  8.8 36.1 %all_to_all.20.got = bf16[32,16,128]{2,1,0:T(8,128)(2,1)S(1)} all-to-all(bf16[32,16,128]{2,1,0:T(8,128)(2,1)S(1)} %get-tuple-element.8), channel_id=1, replica_groups=mesh['row'=16,'col'=32] {'col'}, dimensions={0} | all-to-all | bytes 262144 | tf_op jit(solution)/shard_map/all_to_all | solution.py:163
  45.0 1.6 %copy-done = bf16[1024,1024]{1,0:T(8,128)(2,1)S(1)} copy-done((bf16[1024,1024]{1,0:T(8,128)(2,1)S(1)}, bf16[1024,1024]{1,0:T(8,128)(2,1)}, u32[]{:S(2)}) %copy-start) | copy-done | bytes 2097176
  46.6 0.7 shard_map.146
  47.2 14.4 %all_to_all.21.got = bf16[16,32,128]{2,1,0:T(8,128)(2,1)S(1)} all-to-all(bf16[16,32,128]{2,1,0:T(8,128)(2,1)S(1)} %shard_map.146), channel_id=1, replica_groups=mesh['row'=16,'col'=32] {'row'}, dimensions={0} | all-to-all | bytes 262144 | tf_op jit(solution)/shard_map/all_to_all | solution.py:163
  61.7 0.0 copy-done.9
  61.7 0.0 copy-start.2
  61.7 1.6 %copy-done.2 = bf16[1024,1024]{1,0:T(8,128)(2,1)S(1)} copy-done((bf16[1024,1024]{1,0:T(8,128)(2,1)S(1)}, bf16[1024,1024]{1,0:T(8,128)(2,1)}, u32[]{:S(2)}) %copy-start.2) | copy-done | bytes 2097176
  63.3 1.9 %shard_map.147 = bf16[16,32,128]{2,1,0:T(8,128)(2,1)S(1)} custom-call(f32[32]{0:T(128)S(1)} %copy-done.14, bf16[16,32,128]{2,1,0:T(8,128)(2,1)S(1)} %all_to_all.21.got, bf16[1024,1024]{1,0:T(8,128)(2,1)S(1)} %copy-done.2, f32[8,128]{1,0:T(8,128)S(1)} %bitcast.6, f32[8,128]{1,0:T(8,128)S(1)} %bitcast.7), custom_call_target="tpu_custom_call" | custom-call | tf_op jit(solution)/shard_map/pallas_call | solution.py:152
  65.2 11.2 %all_to_all.22.got = bf16[16,32,128]{2,1,0:T(8,128)(2,1)S(1)} all-to-all(bf16[16,32,128]{2,1,0:T(8,128)(2,1)S(1)} %shard_map.147), channel_id=1, replica_groups=mesh['row'=16,'col'=32] {'row'}, dimensions={0} | all-to-all | bytes 262144 | tf_op jit(solution)/shard_map/all_to_all | solution.py:163
  76.3 1.5 %shard_map.148 = bf16[32,16,128]{2,1,0:T(8,128)(2,1)} custom-call(bf16[16,32,128]{2,1,0:T(8,128)(2,1)S(1)} %all_to_all.22.got, bf16[1024,1024]{1,0:T(8,128)(2,1)S(1)} %copy-done.1), custom_call_target="tpu_custom_call" | custom-call | tf_op jit(solution)/shard_map/pallas_call | solution.py:152
  77.8 5.8 %all-to-all-start.3 = ((bf16[32,16,128]{2,1,0:T(8,128)(2,1)}), bf16[32,16,128]{2,1,0:T(8,128)(2,1)S(1)}, u32[]{:S(2)}, u32[]{:S(2)}) async-start(bf16[32,16,128]{2,1,0:T(8,128)(2,1)} %shard_map.148), calls=%async_computation.3 | async-start | bytes 262144 | tf_op jit(solution)/shard_map/all_to_all | solution.py:163
  83.6 0.1 copy.16.restore
  83.7 15.6 %all-to-all-done.3.got = bf16[32,16,128]{2,1,0:T(8,128)(2,1)S(1)} async-done(((bf16[32,16,128]{2,1,0:T(8,128)(2,1)}), bf16[32,16,128]{2,1,0:T(8,128)(2,1)S(1)}, u32[]{:S(2)}, u32[]{:S(2)}) %all-to-all-start.3) | async-done | bytes 131104 | tf_op jit(solution)/shard_map/all_to_all | solution.py:163
  99.4 1.8 %shard_map.149 = bf16[64,32,64]{2,1,0:T(8,128)(2,1)} custom-call(bf16[32,16,128]{2,1,0:T(8,128)(2,1)S(1)} %all-to-all-done.3.got, bf16[32,16,128]{2,1,0:T(8,128)(2,1)S(1)} %get-tuple-element.9.modal, f32[64,16,128]{2,1,0:T(8,128)S(1)} %get-tuple-element.10.forcing, f32[64,32]{1,0:T(8,128)S(1)} %copy.16.restore), custom_call_target="tpu_custom_call" | custom-call | tf_op jit(solution)/shard_map/pallas_call | solution.py:152
  (19 shorter events, 0.0 us)
Async XLA Ops:
  0.0 61.7 %copy-start.14 = (f32[32]{0:T(128)S(1)}, f32[32]{0:T(128)}, u32[]{:S(2)}) copy-start(f32[32]{0:T(128)} %coupling.1) | copy-start | bytes 388
  0.0 1.1 %copy-start.3 = (bf16[64,32,64]{2,1,0:T(8,128)(2,1)S(1)}, bf16[64,32,64]{2,1,0:T(8,128)(2,1)}, u32[]{:S(2)}) copy-start(bf16[64,32,64]{2,1,0:T(8,128)(2,1)} %temp.1) | copy-start | bytes 786436
  1.1 1.0 %copy-start.4 = (bf16[64,32,64]{2,1,0:T(8,128)(2,1)S(1)}, bf16[64,32,64]{2,1,0:T(8,128)(2,1)}, u32[]{:S(2)}) copy-start(bf16[64,32,64]{2,1,0:T(8,128)(2,1)} %vapour.1) | copy-start | bytes 786436
  2.1 0.7 copy-start.5
  2.8 0.7 copy-start.6
  3.5 0.7 copy-start.7
  4.2 0.7 copy-start.8
  4.9 0.7 copy-start.11
  5.6 0.7 copy-start.12
  6.2 0.7 copy-start.13
  6.9 54.8 %copy-start.9 = (f32[1024]{0:T(1024)S(1)}, f32[1024]{0:T(1024)}, u32[]{:S(2)}) copy-start(f32[1024]{0:T(1024)} %param.27) | copy-start | bytes 12292
  6.9 54.8 %copy-start.10 = (f32[1024]{0:T(1024)S(1)}, f32[1024]{0:T(1024)}, u32[]{:S(2)}) copy-start(f32[1024]{0:T(1024)} %param.28) | copy-start | bytes 12292
  45.0 1.6 %copy-start = (bf16[1024,1024]{1,0:T(8,128)(2,1)S(1)}, bf16[1024,1024]{1,0:T(8,128)(2,1)}, u32[]{:S(2)}) copy-start(bf16[1024,1024]{1,0:T(8,128)(2,1)} %basis.5) | copy-start | bytes 6291460
  46.5 29.8 %copy-start.1 = (bf16[1024,1024]{1,0:T(8,128)(2,1)S(1)}, bf16[1024,1024]{1,0:T(8,128)(2,1)}, u32[]{:S(2)}) copy-start(bf16[1024,1024]{1,0:T(8,128)(2,1)} %basis.5) | copy-start | bytes 6291460
  61.7 1.6 %copy-start.2 = (bf16[1024,1024]{1,0:T(8,128)(2,1)S(1)}, bf16[1024,1024]{1,0:T(8,128)(2,1)}, u32[]{:S(2)}) copy-start(bf16[1024,1024]{1,0:T(8,128)(2,1)} %basis.4) | copy-start | bytes 6291460
  63.3 20.3 %copy-start.15 = (f32[64,32]{0,1:T(8,128)S(1)}, f32[64,32]{0,1:T(8,128)}, u32[]{:S(2)}) copy-start(f32[64,32]{0,1:T(8,128)} %param.22) | copy-start | bytes 24580
  77.8 21.5 %all-to-all-start.3 = ((bf16[32,16,128]{2,1,0:T(8,128)(2,1)}), bf16[32,16,128]{2,1,0:T(8,128)(2,1)S(1)}, u32[]{:S(2)}, u32[]{:S(2)}) async-start(bf16[32,16,128]{2,1,0:T(8,128)(2,1)} %shard_map.148), calls=%async_computation.3 | async-start | bytes 262144 | tf_op jit(solution)/shard_map/all_to_all | solution.py:163

commit v2 on v1

--- a/solution.py
+++ b/solution.py
@@ -9,6 +9,8 @@
 BF16 = jnp.bfloat16
 HALF = 64
 LANES = 128
+GROUPS = 4
+COST = 4_000_000_000
 VMEM_LIMIT = 12 * 1024 * 1024
 
 
@@ -46,10 +48,31 @@
     return jnp.sum(jnp.where(lane == place, jnp.broadcast_to(row, (rows, LANES)), 0.0), axis=1, keepdims=True)
 
 
-def physics(absorb, flux, emission, sunlit, temp, vapour, project, wx, wy, forcing, send, modal, scratch):
+def physics(*refs):
+    sources = refs[:9]
+    forcing, send, modal = refs[9:12]
+    absorb, flux, emission, sunlit, temp, vapour, project, wx, wy = refs[12:21]
+    scratch, done = refs[21:]
     levels = temp.shape[0]
     bands = absorb.shape[0]
     rows = temp.shape[1] // 2
+    group = levels // GROUPS
+    cuts = [pl.ds(k * group, group) for k in range(GROUPS)]
+    copy = pltpu.make_async_copy
+    small = [
+        copy(sources[k], refs[12 + k], done.at[k]) for k in (0, 1, 2, 3, 6, 7, 8)
+    ]
+    large = [
+        [
+            copy(sources[k].at[cut], refs[12 + k].at[cut], done.at[9 + 2 * n + k - 4])
+            for k in (4, 5)
+        ]
+        for n, cut in enumerate(cuts)
+    ]
+    for item in small[:4] + [item for pair in large for item in pair] + small[4:]:
+        item.start()
+    for item in small[:4]:
+        item.wait()
     r = lax.axis_index("row")
     c = lax.axis_index("col")
     shape = (rows, LANES)
@@ -61,6 +84,9 @@
     before = through[0] + through[1] + through[2] + through[3]
     emitted = emission[0] + emission[1] + emission[2] + emission[3]
     for level in range(levels):
+        if level % group == 0:
+            for item in large[level // group]:
+                item.wait()
         t = fold(temp[level]).astype(F32)
         h = fold(vapour[level]).astype(F32)
         kept = None
@@ -73,6 +99,8 @@
             after = through[b] if after is None else after + through[b]
         forcing[level] = t + (before - after) - (emitted - kept) * t
         before = after
+    for item in small[4:]:
+        item.wait()
     left = left_terms(project[...])
     for p in range(0, rows, 2):
         field = jnp.concatenate([forcing[:, p, :], forcing[:, p + 1, :]], axis=1)
@@ -129,7 +157,7 @@
         out[c] = fold(solved[c * rows : (c + 1) * rows])
 
 
-def finish(got, modal, forcing, restore, out, difference, total):
+def finish(got, modal, forcing, restore, target, out, difference, total, done):
     difference[...] = got[...].astype(F32) - modal[...].astype(F32)
     rows = difference.shape[1]
     left = left_terms(restore[...])
@@ -138,24 +166,34 @@
         correction = dot(left, right_terms(field), 1, 0)
         total[:, p, :] = forcing[:, p, :] + correction[:, :LANES]
         total[:, p + 1, :] = forcing[:, p + 1, :] + correction[:, LANES:]
-    for level in range(out.shape[0]):
-        v = total[level].astype(BF16)
-        out[level, :rows, :] = v[:, :HALF]
-        out[level, rows:, :] = v[:, HALF:]
+    group = out.shape[0] // GROUPS
+    copies = []
+    for k in range(GROUPS):
+        cut = pl.ds(k * group, group)
+        for level in range(k * group, (k + 1) * group):
+            v = total[level].astype(BF16)
+            out[level, :rows, :] = v[:, :HALF]
+            out[level, rows:, :] = v[:, HALF:]
+        copies.append(pltpu.make_async_copy(out.at[cut], target.at[cut], done.at[k]))
+        copies[k].start()
+    for item in copies:
+        item.wait()
 
 
 SMEM = pl.BlockSpec(memory_space=pltpu.SMEM)
 VMEM = pl.BlockSpec(memory_space=pltpu.VMEM)
-
-
-def call(body, smem, vmem, outs, scratch, *operands):
+HBM = pl.BlockSpec(memory_space=pltpu.HBM)
+
+
+def call(body, in_specs, out_specs, outs, scratch, *operands):
     return pl.pallas_call(
         body,
-        in_specs=[SMEM] * smem + [VMEM] * vmem,
-        out_specs=[VMEM] * len(outs),
+        in_specs=in_specs,
+        out_specs=out_specs,
         out_shape=[jax.ShapeDtypeStruct(shape, dtype) for shape, dtype in outs],
-        scratch_shapes=[pltpu.VMEM(shape, dtype) for shape, dtype in scratch],
+        scratch_shapes=scratch,
         compiler_params=pltpu.CompilerParams(vmem_limit_bytes=VMEM_LIMIT),
+        cost_estimate=pl.CostEstimate(flops=COST, bytes_accessed=COST // 1000, transcendentals=0),
     )(*operands)
 
 
@@ -187,12 +225,7 @@
     tile = (rows, LANES)
     block = (HALF // 2, LANES)
     lanes = lambda v: v.reshape(-1, LANES)
-    forcing, send, modal = call(
-        physics,
-        4,
-        5,
-        [((levels, *tile), F32), ((modes, *tile), BF16), ((modes, *tile), BF16)],
-        [((modes, *tile), F32)],
+    sources = (
         absorb,
         solar_flux,
         emission,
@@ -203,26 +236,46 @@
         lanes(east_weight),
         lanes(north_weight),
     )
-    (send,) = call(to_east, 0, 2, [((n_row, *block), BF16)], [], exchange(send, "col"), east_basis)
+    held = [pltpu.SMEM] * 4 + [pltpu.VMEM] * 5
+    forcing, send, modal = call(
+        physics,
+        [HBM] * 9,
+        [VMEM] * 3,
+        [((levels, *tile), F32), ((modes, *tile), BF16), ((modes, *tile), BF16)],
+        [space(v.shape, v.dtype) for space, v in zip(held, sources)]
+        + [pltpu.VMEM((modes, *tile), F32), pltpu.SemaphoreType.DMA((9 + 2 * GROUPS,))],
+        *(pltpu.with_memory_space_constraint(v, pltpu.HBM) for v in sources),
+    )
+    (send,) = call(
+        to_east, [VMEM] * 2, [VMEM], [((n_row, *block), BF16)], [], exchange(send, "col"), east_basis
+    )
     (send,) = call(
         solve,
-        1,
-        4,
+        [SMEM] + [VMEM] * 4,
+        [VMEM],
         [((n_row, *block), BF16)],
-        [((HALF, north_basis.shape[0]), BF16)],
+        [pltpu.VMEM((HALF, north_basis.shape[0]), BF16)],
         coupling,
         exchange(send, "row"),
         north_basis,
         lanes(east_eigen),
         lanes(north_eigen),
     )
-    (send,) = call(from_east, 0, 2, [((modes, *tile), BF16)], [], exchange(send, "row"), east_basis)
+    (send,) = call(
+        from_east, [VMEM] * 2, [VMEM], [((modes, *tile), BF16)], [], exchange(send, "row"), east_basis
+    )
+    shape = (levels, east_local, north_local)
     (out,) = call(
         finish,
-        0,
-        4,
-        [((levels, east_local, north_local), BF16)],
-        [((modes, *tile), F32), ((levels, *tile), F32)],
+        [VMEM] * 4,
+        [HBM],
+        [(shape, BF16)],
+        [
+            pltpu.VMEM(shape, BF16),
+            pltpu.VMEM((modes, *tile), F32),
+            pltpu.VMEM((levels, *tile), F32),
+            pltpu.SemaphoreType.DMA((GROUPS,)),
+        ],
         exchange(send, "col"),
         modal,
         forcing,

time: 102 us -> 92.5 us (0.907)
  local copies, waits for them, and re-layouts: 10.1 us -> 0.1 us
    unnamed x33 -> x13, local copies, waits for them, and re-layouts: 10.1 us -> 0.1 us
where the time goes in v2:
time: 92.5 us; the launch traced here: 91.7 us
  blocking collectives  61.7 us (67%)
  waiting for transfers between devices  15.6 us (17%)
  Pallas kernels  8.43 us (9%)
  starting transfers between devices  5.79 us (6%)
    all_to_all x3, blocking collectives, exchange(): return lax.all_to_all(v, axis, split_axis=0, concat_axis=0, tiled=True)  61.7 us
    all_to_all x1, waiting for transfers between devices, exchange(): return lax.all_to_all(v, axis, split_axis=0, concat_axis=0, tiled=True)  15.6 us
    pallas_call x5, Pallas kernels, call(): pl.pallas_call(body, in_specs=in_specs, out_specs=out_specs, out_shape=[j...  8.43 us
    all_to_all x1, starting transfers between devices, exchange(): return lax.all_to_all(v, axis, split_axis=0, concat_axis=0, tiled=True)  5.79 us
  transfers between devices with their start and end apart: 1, of which 1 were waited for; matrix products, arithmetic and copies ran while one was open for 0% of the time, Pallas kernels for 0%

profile of v2, /device:TPU:1, one launch (start us, length us, event | category | flops | bytes accessed | tf_op | source)
XLA Modules:
  0.0 91.7 jit_solution(10043890171236293553)
XLA Ops:
  0.0 0.0 copy-start.1
  0.0 2.7 %shard_map.145 = (f32[64,16,128]{2,1,0:T(8,128)S(1)}, bf16[32,16,128]{2,1,0:T(8,128)(2,1)S(1)}, bf16[32,16,128]{2,1,0:T(8,128)(2,1)S(1)}) custom-call(f32[4,64]{1,0:T(4,128)} %refs_0_.1, f32[4]{0:T(128)} %refs_1_.1, f32[4]{0:T(128)} %refs_2_.1, s32[16,32]{1,0:T(8,128)} %refs_3_.1, bf16[64,32,64]{2,1,0:T(8,128)(2,1)} %refs_4_.1, bf16[64,32,64]{2,1,0:T(8,128)(2,1)} %refs_5_.1, ...), custom_call_target="tpu_custom_call" | custom-call | flops 4000000000 | bytes 4000000 | tf_op jit(solution)/shard_map/pallas_call | solution.py:189
  2.7 36.1 %all_to_all.20.got = bf16[32,16,128]{2,1,0:T(8,128)(2,1)S(1)} all-to-all(bf16[32,16,128]{2,1,0:T(8,128)(2,1)S(1)} %get-tuple-element.8), channel_id=1, replica_groups=mesh['row'=16,'col'=32] {'col'}, dimensions={0} | all-to-all | bytes 262144 | tf_op jit(solution)/shard_map/all_to_all | solution.py:201
  38.8 0.0 copy-done.1
  38.8 0.0 copy-start
  38.8 0.0 copy-start.2
  38.8 0.0 copy-start.3
  38.8 0.0 copy-start.4
  38.8 0.7 shard_map.146
  39.5 14.4 %all_to_all.21.got = bf16[16,32,128]{2,1,0:T(8,128)(2,1)S(1)} all-to-all(bf16[16,32,128]{2,1,0:T(8,128)(2,1)S(1)} %shard_map.146), channel_id=1, replica_groups=mesh['row'=16,'col'=32] {'row'}, dimensions={0} | all-to-all | bytes 262144 | tf_op jit(solution)/shard_map/all_to_all | solution.py:201
  54.0 0.0 copy-done
  54.0 0.0 copy-done.2
  54.0 0.0 copy-done.3
  54.0 0.0 copy-done.4
  54.0 1.9 %shard_map.147 = bf16[16,32,128]{2,1,0:T(8,128)(2,1)S(1)} custom-call(f32[32]{0:T(128)S(1)} %copy-done.4, bf16[16,32,128]{2,1,0:T(8,128)(2,1)S(1)} %all_to_all.21.got, bf16[1024,1024]{1,0:T(8,128)(2,1)S(1)} %copy-done, f32[8,128]{1,0:T(8,128)S(1)} %bitcast.4, f32[8,128]{1,0:T(8,128)S(1)} %bitcast.5), custom_call_target="tpu_custom_call" | custom-call | flops 4000000000 | bytes 4000000 | tf_op jit(solution)/shard_map/pallas_call | solution.py:189
  55.9 11.2 %all_to_all.22.got = bf16[16,32,128]{2,1,0:T(8,128)(2,1)S(1)} all-to-all(bf16[16,32,128]{2,1,0:T(8,128)(2,1)S(1)} %shard_map.147), channel_id=1, replica_groups=mesh['row'=16,'col'=32] {'row'}, dimensions={0} | all-to-all | bytes 262144 | tf_op jit(solution)/shard_map/all_to_all | solution.py:201
  67.0 0.0 copy-start.5
  67.0 1.5 %shard_map.148 = bf16[32,16,128]{2,1,0:T(8,128)(2,1)} custom-call(bf16[16,32,128]{2,1,0:T(8,128)(2,1)S(1)} %all_to_all.22.got, bf16[1024,1024]{1,0:T(8,128)(2,1)S(1)} %copy-done.1), custom_call_target="tpu_custom_call" | custom-call | flops 4000000000 | bytes 4000000 | tf_op jit(solution)/shard_map/pallas_call | solution.py:189
  68.5 5.8 %all-to-all-start.3 = ((bf16[32,16,128]{2,1,0:T(8,128)(2,1)}), bf16[32,16,128]{2,1,0:T(8,128)(2,1)S(1)}, u32[]{:S(2)}, u32[]{:S(2)}) async-start(bf16[32,16,128]{2,1,0:T(8,128)(2,1)} %shard_map.148), calls=%async_computation.3 | async-start | bytes 262144 | tf_op jit(solution)/shard_map/all_to_all | solution.py:201
  74.3 0.0 copy-done.5
  74.3 0.1 copy.16.restore
  74.4 15.6 %all-to-all-done.3.got = bf16[32,16,128]{2,1,0:T(8,128)(2,1)S(1)} async-done(((bf16[32,16,128]{2,1,0:T(8,128)(2,1)}), bf16[32,16,128]{2,1,0:T(8,128)(2,1)S(1)}, u32[]{:S(2)}, u32[]{:S(2)}) %all-to-all-start.3) | async-done | bytes 131104 | tf_op jit(solution)/shard_map/all_to_all | solution.py:201
  90.1 1.7 %shard_map.149 = bf16[64,32,64]{2,1,0:T(8,128)(2,1)} custom-call(bf16[32,16,128]{2,1,0:T(8,128)(2,1)S(1)} %all-to-all-done.3.got, bf16[32,16,128]{2,1,0:T(8,128)(2,1)S(1)} %get-tuple-element.9.modal, f32[64,16,128]{2,1,0:T(8,128)S(1)} %get-tuple-element.10.forcing, f32[64,32]{1,0:T(8,128)S(1)} %copy.16.restore), custom_call_target="tpu_custom_call" | custom-call | flops 4000000000 | bytes 4000000 | tf_op jit(solution)/shard_map/pallas_call | solution.py:189
Async XLA Ops:
  0.0 38.8 %copy-start.1 = (bf16[1024,1024]{1,0:T(8,128)(2,1)S(1)}, bf16[1024,1024]{1,0:T(8,128)(2,1)}, u32[]{:S(2)}) copy-start(bf16[1024,1024]{1,0:T(8,128)(2,1)} %basis.5) | copy-start | bytes 6291460
  38.8 15.2 %copy-start = (bf16[1024,1024]{1,0:T(8,128)(2,1)S(1)}, bf16[1024,1024]{1,0:T(8,128)(2,1)}, u32[]{:S(2)}) copy-start(bf16[1024,1024]{1,0:T(8,128)(2,1)} %basis.4) | copy-start | bytes 6291460
  38.8 15.2 %copy-start.2 = (f32[1024]{0:T(1024)S(1)}, f32[1024]{0:T(1024)}, u32[]{:S(2)}) copy-start(f32[1024]{0:T(1024)} %param.27) | copy-start | bytes 12292
  38.8 15.2 %copy-start.3 = (f32[1024]{0:T(1024)S(1)}, f32[1024]{0:T(1024)}, u32[]{:S(2)}) copy-start(f32[1024]{0:T(1024)} %param.28) | copy-start | bytes 12292
  38.8 15.2 %copy-start.4 = (f32[32]{0:T(128)S(1)}, f32[32]{0:T(128)}, u32[]{:S(2)}) copy-start(f32[32]{0:T(128)} %coupling.1) | copy-start | bytes 388
  67.0 7.3 %copy-start.5 = (f32[64,32]{0,1:T(8,128)S(1)}, f32[64,32]{0,1:T(8,128)}, u32[]{:S(2)}) copy-start(f32[64,32]{0,1:T(8,128)} %param.22) | copy-start | bytes 24580
  68.5 21.5 %all-to-all-start.3 = ((bf16[32,16,128]{2,1,0:T(8,128)(2,1)}), bf16[32,16,128]{2,1,0:T(8,128)(2,1)S(1)}, u32[]{:S(2)}, u32[]{:S(2)}) async-start(bf16[32,16,128]{2,1,0:T(8,128)(2,1)} %shard_map.148), calls=%async_computation.3 | async-start | bytes 262144 | tf_op jit(solution)/shard_map/all_to_all | solution.py:201

commit v3 on v2

--- a/solution.py
+++ b/solution.py
@@ -9,7 +9,8 @@
 BF16 = jnp.bfloat16
 HALF = 64
 LANES = 128
-GROUPS = 4
+GROUPS = 2
+MINUS_LOG2_E = -1.4426950408889634
 COST = 4_000_000_000
 VMEM_LIMIT = 12 * 1024 * 1024
 
@@ -46,6 +47,15 @@
 def column_of(row, first, rows, lane):
     place = lax.broadcasted_iota(jnp.int32, (rows, LANES), 0) + first
     return jnp.sum(jnp.where(lane == place, jnp.broadcast_to(row, (rows, LANES)), 0.0), axis=1, keepdims=True)
+
+
+def pair_of(ref, p, count, rows):
+    return jnp.concatenate([ref[pl.ds(p + k, count, stride=rows), :] for k in (0, 1)], axis=1)
+
+
+def set_pair(ref, p, value, rows):
+    for k in (0, 1):
+        ref[pl.ds(p + k, value.shape[0], stride=rows), :] = value[:, k * LANES : (k + 1) * LANES]
 
 
 def physics(*refs):
@@ -88,25 +98,23 @@
             for item in large[level // group]:
                 item.wait()
         t = fold(temp[level]).astype(F32)
-        h = fold(vapour[level]).astype(F32)
+        h = fold(vapour[level]).astype(F32) * MINUS_LOG2_E
         kept = None
         after = None
         for b in range(bands):
-            pass_through = jnp.exp(h * (-absorb[b, level]))
+            pass_through = jnp.exp2(h * absorb[b, level])
             through[b] = through[b] * pass_through
             part = pass_through * emission[b]
             kept = part if kept is None else kept + part
             after = through[b] if after is None else after + through[b]
-        forcing[level] = t + (before - after) - (emitted - kept) * t
+        forcing[level * rows : (level + 1) * rows, :] = t + (before - after) - (emitted - kept) * t
         before = after
     for item in small[4:]:
         item.wait()
     left = left_terms(project[...])
     for p in range(0, rows, 2):
-        field = jnp.concatenate([forcing[:, p, :], forcing[:, p + 1, :]], axis=1)
-        out = dot(left, right_terms(field), 1, 0)
-        scratch[:, p, :] = out[:, :LANES]
-        scratch[:, p + 1, :] = out[:, LANES:]
+        out = dot(left, right_terms(pair_of(forcing, p, levels, rows)), 1, 0)
+        set_pair(scratch, p, out, rows)
     per_row = LANES // (2 * rows)
     x_row = wx[pl.ds(c // per_row, 1), :]
     first = (c % per_row) * (2 * rows)
@@ -115,7 +123,7 @@
     y_row = jnp.broadcast_to(y_row, shape)
     north = jnp.where(upper == (r % 2 == 1), y_row, pltpu.roll(y_row, HALF, 1))
     weight = east * north
-    field = scratch[...]
+    field = scratch[...].reshape(modal.shape)
     modal[...] = field.astype(BF16)
     send[...] = (field * weight[None]).astype(BF16)
 
@@ -129,6 +137,15 @@
         out[2 * b + 1] = jnp.concatenate([top[:, HALF:], low[:, HALF:]], axis=1)
 
 
+def gather_blocks(got, wide):
+    n = got.shape[1]
+    for b in range(got.shape[0] // 2):
+        one, two = got[2 * b], got[2 * b + 1]
+        place = slice(b * LANES, (b + 1) * LANES)
+        wide[:n, place] = jnp.concatenate([one[:, :HALF], two[:, :HALF]], axis=1)
+        wide[n:, place] = jnp.concatenate([one[:, HALF:], two[:, HALF:]], axis=1)
+
+
 def to_east(got, basis, out):
     wide = dot(unfold(got[...]), basis[...], 0, 0).astype(BF16)
     scatter_blocks(wide, out)
@@ -137,7 +154,8 @@
 def solve(coupling, got, basis, east, north, out, scaled):
     r = lax.axis_index("row")
     c = lax.axis_index("col")
-    gravity = coupling[c]
+    place = lax.broadcasted_iota(jnp.int32, coupling.shape, 1)
+    gravity = jnp.sum(jnp.where(place == c, coupling[...], 0.0), axis=1, keepdims=True)
     mine = unfold(got[...])
     spectral = dot(mine, basis[...], 0, 0)
     n = spectral.shape[0]
@@ -146,32 +164,36 @@
     for b in range(spectral.shape[1] // LANES):
         divisor = 1.0 + gravity * (roots + north[b : b + 1, :])
         scaled[:, b * LANES : (b + 1) * LANES] = (spectral[:, b * LANES : (b + 1) * LANES] / divisor).astype(BF16)
-    wide = dot(scaled[...], basis[...], 1, 1).astype(BF16)
-    scatter_blocks(wide, out)
-
-
-def from_east(got, basis, out):
-    solved = dot(basis[...], unfold(got[...]), 1, 0).astype(BF16)
+    tall = dot(basis[...], scaled[...], 1, 1).astype(BF16)
+    for b in range(out.shape[0]):
+        out[b] = fold(tall[b * HALF : (b + 1) * HALF])
+
+
+def from_east(got, basis, out, wide):
+    gather_blocks(got, wide)
+    solved = dot(basis[...], wide[...], 1, 1).astype(BF16)
     rows = 2 * out.shape[1]
     for c in range(out.shape[0]):
         out[c] = fold(solved[c * rows : (c + 1) * rows])
 
 
 def finish(got, modal, forcing, restore, target, out, difference, total, done):
-    difference[...] = got[...].astype(F32) - modal[...].astype(F32)
-    rows = difference.shape[1]
-    left = left_terms(restore[...])
+    modes, rows, _ = got.shape
+    levels = out.shape[0]
+    gap = got[...].astype(F32) - modal[...].astype(F32)
+    difference[...] = gap.reshape(difference.shape)
+    high, low = halves(restore[...])
+    left = jnp.concatenate([high, low, high], axis=0)
     for p in range(0, rows, 2):
-        field = jnp.concatenate([difference[:, p, :], difference[:, p + 1, :]], axis=1)
-        correction = dot(left, right_terms(field), 1, 0)
-        total[:, p, :] = forcing[:, p, :] + correction[:, :LANES]
-        total[:, p + 1, :] = forcing[:, p + 1, :] + correction[:, LANES:]
-    group = out.shape[0] // GROUPS
+        correction = dot(left, right_terms(pair_of(difference, p, modes, rows)), 0, 0)
+        set_pair(total, p, correction, rows)
+    group = levels // GROUPS
     copies = []
     for k in range(GROUPS):
         cut = pl.ds(k * group, group)
         for level in range(k * group, (k + 1) * group):
-            v = total[level].astype(BF16)
+            here = slice(level * rows, (level + 1) * rows)
+            v = (forcing[here, :] + total[here, :]).astype(BF16)
             out[level, :rows, :] = v[:, :HALF]
             out[level, rows:, :] = v[:, HALF:]
         copies.append(pltpu.make_async_copy(out.at[cut], target.at[cut], done.at[k]))
@@ -241,9 +263,9 @@
         physics,
         [HBM] * 9,
         [VMEM] * 3,
-        [((levels, *tile), F32), ((modes, *tile), BF16), ((modes, *tile), BF16)],
+        [((levels * rows, LANES), F32), ((modes, *tile), BF16), ((modes, *tile), BF16)],
         [space(v.shape, v.dtype) for space, v in zip(held, sources)]
-        + [pltpu.VMEM((modes, *tile), F32), pltpu.SemaphoreType.DMA((9 + 2 * GROUPS,))],
+        + [pltpu.VMEM((modes * rows, LANES), F32), pltpu.SemaphoreType.DMA((9 + 2 * GROUPS,))],
         *(pltpu.with_memory_space_constraint(v, pltpu.HBM) for v in sources),
     )
     (send,) = call(
@@ -251,18 +273,24 @@
     )
     (send,) = call(
         solve,
-        [SMEM] + [VMEM] * 4,
+        [VMEM] * 5,
         [VMEM],
         [((n_row, *block), BF16)],
         [pltpu.VMEM((HALF, north_basis.shape[0]), BF16)],
-        coupling,
+        coupling.reshape(1, -1),
         exchange(send, "row"),
         north_basis,
         lanes(east_eigen),
         lanes(north_eigen),
     )
     (send,) = call(
-        from_east, [VMEM] * 2, [VMEM], [((modes, *tile), BF16)], [], exchange(send, "row"), east_basis
+        from_east,
+        [VMEM] * 2,
+        [VMEM],
+        [((modes, *tile), BF16)],
+        [pltpu.VMEM((HALF, east_basis.shape[0]), BF16)],
+        exchange(send, "row"),
+        east_basis,
     )
     shape = (levels, east_local, north_local)
     (out,) = call(
@@ -272,14 +300,14 @@
         [(shape, BF16)],
         [
             pltpu.VMEM(shape, BF16),
-            pltpu.VMEM((modes, *tile), F32),
-            pltpu.VMEM((levels, *tile), F32),
+            pltpu.VMEM((modes * rows, LANES), F32),
+            pltpu.VMEM((levels * rows, LANES), F32),
             pltpu.SemaphoreType.DMA((GROUPS,)),
         ],
         exchange(send, "col"),
         modal,
         forcing,
-        restore,
+        restore.T,
     )
     return out
 

time: 92.5 us -> 89.7 us (0.970)
  blocking collectives: 61.7 us -> 82.4 us
  waiting for transfers between devices: 15.6 us -> 0 us
  starting transfers between devices: 5.79 us -> 0 us
  Pallas kernels: 8.43 us -> 6.51 us
    all_to_all x3 -> x4, blocking collectives: 61.7 us -> 82.4 us  [exchange(): return lax.all_to_all(v, axis, split_axis=0, concat_axis=0, tiled=True)]
    all_to_all x1 -> x0, waiting for transfers between devices: 15.6 us -> none  [exchange(): return lax.all_to_all(v, axis, split_axis=0, concat_axis=0, tiled=True)]
    all_to_all x1 -> x0, starting transfers between devices: 5.79 us -> none  [exchange(): return lax.all_to_all(v, axis, split_axis=0, concat_axis=0, tiled=True)]
    pallas_call x5, Pallas kernels: 8.43 us -> 6.51 us  [call(): pl.pallas_call(body, in_specs=in_specs, out_specs=out_specs, out_shape=[j...]
  transfers between devices with their start and end apart: 1 -> 0, of which waited for: 1 -> 0; matrix products, arithmetic and copies ran while one was open for 0% -> 0% of each run, Pallas kernels for 0% -> 0%
where the time goes in v3:
time: 89.7 us; the launch traced here: 89 us
  blocking collectives  82.4 us (92%)
  Pallas kernels  6.51 us (7%)
    all_to_all x4, blocking collectives, exchange(): return lax.all_to_all(v, axis, split_axis=0, concat_axis=0, tiled=True)  82.4 us
    pallas_call x5, Pallas kernels, call(): pl.pallas_call(body, in_specs=in_specs, out_specs=out_specs, out_shape=[j...  6.51 us

profile of v3, /device:TPU:1, one launch (start us, length us, event | category | flops | bytes accessed | tf_op | source)
XLA Modules:
  0.0 89.0 jit_solution(6776478330322413837)
XLA Ops:
  0.0 0.0 copy-start.1
  0.0 2.4 %shard_map.145 = (f32[1024,128]{1,0:T(8,128)S(1)}, bf16[32,16,128]{2,1,0:T(8,128)(2,1)S(1)}, bf16[32,16,128]{2,1,0:T(8,128)(2,1)S(1)}) custom-call(f32[4,64]{1,0:T(4,128)} %refs_0_.1, f32[4]{0:T(128)} %refs_1_.1, f32[4]{0:T(128)} %refs_2_.1, s32[16,32]{1,0:T(8,128)} %refs_3_.1, bf16[64,32,64]{2,1,0:T(8,128)(2,1)} %refs_4_.1, bf16[64,32,64]{2,1,0:T(8,128)(2,1)} %refs_5_.1, ...), custom_call_target="tpu_custom_call" | custom-call | flops 4000000000 | bytes 4000000 | tf_op jit(solution)/shard_map/pallas_call | solution.py:211
  2.4 36.1 %all_to_all.20.got = bf16[32,16,128]{2,1,0:T(8,128)(2,1)S(1)} all-to-all(bf16[32,16,128]{2,1,0:T(8,128)(2,1)S(1)} %get-tuple-element.8), channel_id=1, replica_groups=mesh['row'=16,'col'=32] {'col'}, dimensions={0} | all-to-all | bytes 262144 | tf_op jit(solution)/shard_map/all_to_all | solution.py:223
  38.5 0.0 copy-done.1
  38.5 0.0 copy-start
  38.5 0.0 copy-start.3
  38.5 0.0 copy-start.4
  38.5 0.0 copy-start.5
  38.5 0.7 shard_map.146
  39.2 14.4 %all_to_all.21.got = bf16[16,32,128]{2,1,0:T(8,128)(2,1)S(1)} all-to-all(bf16[16,32,128]{2,1,0:T(8,128)(2,1)S(1)} %shard_map.146), channel_id=1, replica_groups=mesh['row'=16,'col'=32] {'row'}, dimensions={0} | all-to-all | bytes 262144 | tf_op jit(solution)/shard_map/all_to_all | solution.py:223
  53.7 0.0 copy-done
  53.7 0.0 copy-done.3
  53.7 0.0 copy-done.4
  53.7 0.0 copy-done.5
  53.7 1.4 %shard_map.147 = bf16[16,32,128]{2,1,0:T(8,128)(2,1)S(1)} custom-call(f32[1,32]{1,0:T(1,128)S(1)} %bitcast.9, bf16[16,32,128]{2,1,0:T(8,128)(2,1)S(1)} %all_to_all.21.got, bf16[1024,1024]{1,0:T(8,128)(2,1)S(1)} %copy-done, f32[8,128]{1,0:T(8,128)S(1)} %bitcast.7, f32[8,128]{1,0:T(8,128)S(1)} %bitcast.8), custom_call_target="tpu_custom_call" | custom-call | flops 4000000000 | bytes 4000000 | tf_op jit(solution)/shard_map/pallas_call | solution.py:211
  55.0 11.2 %all_to_all.22.got = bf16[16,32,128]{2,1,0:T(8,128)(2,1)S(1)} all-to-all(bf16[16,32,128]{2,1,0:T(8,128)(2,1)S(1)} %shard_map.147), channel_id=1, replica_groups=mesh['row'=16,'col'=32] {'row'}, dimensions={0} | all-to-all | bytes 262144 | tf_op jit(solution)/shard_map/all_to_all | solution.py:223
  66.2 0.0 copy-start.2
  66.2 0.8 shard_map.148
  67.0 20.7 %all_to_all.23.got = bf16[32,16,128]{2,1,0:T(8,128)(2,1)S(1)} all-to-all(bf16[32,16,128]{2,1,0:T(8,128)(2,1)S(1)} %shard_map.148), channel_id=1, replica_groups=mesh['row'=16,'col'=32] {'col'}, dimensions={0} | all-to-all | bytes 262144 | tf_op jit(solution)/shard_map/all_to_all | solution.py:223
  87.7 0.0 copy-done.2
  87.7 1.3 %shard_map.149 = bf16[64,32,64]{2,1,0:T(8,128)(2,1)} custom-call(bf16[32,16,128]{2,1,0:T(8,128)(2,1)S(1)} %all_to_all.23.got, bf16[32,16,128]{2,1,0:T(8,128)(2,1)S(1)} %get-tuple-element.9.modal, f32[1024,128]{1,0:T(8,128)S(1)} %get-tuple-element.10.forcing, f32[32,64]{1,0:T(8,128)S(1)} %bitcast.6), custom_call_target="tpu_custom_call" | custom-call | flops 4000000000 | bytes 4000000 | tf_op jit(solution)/shard_map/pallas_call | solution.py:211
Async XLA Ops:
  0.0 38.5 %copy-start.1 = (bf16[1024,1024]{1,0:T(8,128)(2,1)S(1)}, bf16[1024,1024]{1,0:T(8,128)(2,1)}, u32[]{:S(2)}) copy-start(bf16[1024,1024]{1,0:T(8,128)(2,1)} %basis.5) | copy-start | bytes 6291460
  38.5 15.2 %copy-start = (bf16[1024,1024]{1,0:T(8,128)(2,1)S(1)}, bf16[1024,1024]{1,0:T(8,128)(2,1)}, u32[]{:S(2)}) copy-start(bf16[1024,1024]{1,0:T(8,128)(2,1)} %basis.4) | copy-start | bytes 6291460
  38.5 15.2 %copy-start.3 = (f32[1024]{0:T(1024)S(1)}, f32[1024]{0:T(1024)}, u32[]{:S(2)}) copy-start(f32[1024]{0:T(1024)} %param.27) | copy-start | bytes 12292
  38.5 15.2 %copy-start.4 = (f32[1024]{0:T(1024)S(1)}, f32[1024]{0:T(1024)}, u32[]{:S(2)}) copy-start(f32[1024]{0:T(1024)} %param.28) | copy-start | bytes 12292
  38.5 15.2 %copy-start.5 = (f32[32]{0:T(128)S(1)}, f32[32]{0:T(128)}, u32[]{:S(2)}) copy-start(f32[32]{0:T(128)} %param.29) | copy-start | bytes 388
  66.2 21.5 %copy-start.2 = (f32[64,32]{0,1:T(8,128)S(1)}, f32[64,32]{0,1:T(8,128)}, u32[]{:S(2)}) copy-start(f32[64,32]{0,1:T(8,128)} %param.22) | copy-start | bytes 24580

commit v4 on v3

--- a/solution.py
+++ b/solution.py
@@ -11,6 +11,8 @@
 LANES = 128
 GROUPS = 2
 MINUS_LOG2_E = -1.4426950408889634
+COL_MASK = 21
+ROW_MASK = 6
 COST = 4_000_000_000
 VMEM_LIMIT = 12 * 1024 * 1024
 
@@ -24,8 +26,9 @@
     return jnp.concatenate([v[:n], v[n:]], axis=1)
 
 
-def unfold(v):
-    k, n, _ = v.shape
+def unfold(ref, mask):
+    k, n, _ = ref.shape
+    v = jnp.stack([ref[b ^ mask] for b in range(k)], axis=0)
     return jnp.concatenate([v[:, :, :HALF], v[:, :, HALF:]], axis=1).reshape(k * 2 * n, HALF)
 
 
@@ -147,16 +150,16 @@
 
 
 def to_east(got, basis, out):
-    wide = dot(unfold(got[...]), basis[...], 0, 0).astype(BF16)
+    wide = dot(unfold(got, COL_MASK), basis[...], 0, 0).astype(BF16)
     scatter_blocks(wide, out)
 
 
 def solve(coupling, got, basis, east, north, out, scaled):
-    r = lax.axis_index("row")
-    c = lax.axis_index("col")
+    r = lax.axis_index("row") ^ ROW_MASK
+    c = lax.axis_index("col") ^ COL_MASK
     place = lax.broadcasted_iota(jnp.int32, coupling.shape, 1)
     gravity = jnp.sum(jnp.where(place == c, coupling[...], 0.0), axis=1, keepdims=True)
-    mine = unfold(got[...])
+    mine = unfold(got, ROW_MASK)
     spectral = dot(mine, basis[...], 0, 0)
     n = spectral.shape[0]
     lane = lax.broadcasted_iota(jnp.int32, (n, LANES), 1)
@@ -166,7 +169,7 @@
         scaled[:, b * LANES : (b + 1) * LANES] = (spectral[:, b * LANES : (b + 1) * LANES] / divisor).astype(BF16)
     tall = dot(basis[...], scaled[...], 1, 1).astype(BF16)
     for b in range(out.shape[0]):
-        out[b] = fold(tall[b * HALF : (b + 1) * HALF])
+        out[b ^ ROW_MASK] = fold(tall[b * HALF : (b + 1) * HALF])
 
 
 def from_east(got, basis, out, wide):
@@ -174,7 +177,7 @@
     solved = dot(basis[...], wide[...], 1, 1).astype(BF16)
     rows = 2 * out.shape[1]
     for c in range(out.shape[0]):
-        out[c] = fold(solved[c * rows : (c + 1) * rows])
+        out[c ^ COL_MASK] = fold(solved[c * rows : (c + 1) * rows])
 
 
 def finish(got, modal, forcing, restore, target, out, difference, total, done):
@@ -220,7 +223,9 @@
 
 
 def exchange(v, axis):
-    return lax.all_to_all(v, axis, split_axis=0, concat_axis=0, tiled=True)
+    mask = COL_MASK if axis == "col" else ROW_MASK
+    order = [k ^ mask for k in range(v.shape[0])]
+    return lax.all_to_all(v, axis, split_axis=0, concat_axis=0, tiled=True, axis_index_groups=[order])
 
 
 def local(

time: 89.7 us -> 77.8 us (0.87)
  blocking collectives: 82.4 us -> 71 us
    all_to_all x4, blocking collectives: 82.4 us -> 71 us  [exchange(): lax.all_to_all(v, axis, split_axis=0, concat_axis=0, tiled=True, axis_ind...]
where the time goes in v4:
time: 77.8 us; the launch traced here: 77.5 us
  blocking collectives  71 us (91%)
  Pallas kernels  6.52 us (8%)
    all_to_all x4, blocking collectives, exchange(): lax.all_to_all(v, axis, split_axis=0, concat_axis=0, tiled=True, axis_ind...  71 us
    pallas_call x5, Pallas kernels, call(): pl.pallas_call(body, in_specs=in_specs, out_specs=out_specs, out_shape=[j...  6.52 us

profile of v4, /device:TPU:1, one launch (start us, length us, event | category | flops | bytes accessed | tf_op | source)
XLA Modules:
  0.0 77.5 jit_solution(1948266230030392701)
XLA Ops:
  0.0 0.0 copy-start.1
  0.0 2.4 %shard_map.145 = (f32[1024,128]{1,0:T(8,128)S(1)}, bf16[32,16,128]{2,1,0:T(8,128)(2,1)S(1)}, bf16[32,16,128]{2,1,0:T(8,128)(2,1)S(1)}) custom-call(f32[4,64]{1,0:T(4,128)} %refs_0_.1, f32[4]{0:T(128)} %refs_1_.1, f32[4]{0:T(128)} %refs_2_.1, s32[16,32]{1,0:T(8,128)} %refs_3_.1, bf16[64,32,64]{2,1,0:T(8,128)(2,1)} %refs_4_.1, bf16[64,32,64]{2,1,0:T(8,128)(2,1)} %refs_5_.1, ...), custom_call_target="tpu_custom_call" | custom-call | flops 4000000000 | bytes 4000000 | tf_op jit(solution)/shard_map/pallas_call | solution.py:214
  2.4 27.2 %all_to_all.20.got = bf16[32,16,128]{2,1,0:T(8,128)(2,1)S(1)} all-to-all(bf16[32,16,128]{2,1,0:T(8,128)(2,1)S(1)} %get-tuple-element.8), channel_id=1, replica_groups={{21,20,23,22,17,16,19,18,29,28,31,30,25,24,27,26,5,4,7,6,1,0,3,2,13,12,..., dimensions={0} | all-to-all | bytes 262144 | tf_op jit(solution)/shard_map/all_to_all | solution.py:228
  29.5 0.0 copy-done.1
  29.5 0.0 copy-start
  29.5 0.0 copy-start.3
  29.5 0.0 copy-start.4
  29.6 0.0 copy-start.5
  29.6 0.7 shard_map.146
  30.3 11.2 %all_to_all.21.got = bf16[16,32,128]{2,1,0:T(8,128)(2,1)S(1)} all-to-all(bf16[16,32,128]{2,1,0:T(8,128)(2,1)S(1)} %shard_map.146), channel_id=1, replica_groups={{192,224,128,160,64,96,0,32,448,480,384,416,320,352,256,288},{193,225,1..., dimensions={0} | all-to-all | bytes 262144 | tf_op jit(solution)/shard_map/all_to_all | solution.py:228
  41.4 0.0 copy-done
  41.4 0.0 copy-done.3
  41.5 0.0 copy-done.4
  41.5 0.0 copy-done.5
  41.5 1.4 %shard_map.147 = bf16[16,32,128]{2,1,0:T(8,128)(2,1)S(1)} custom-call(f32[1,32]{1,0:T(1,128)S(1)} %bitcast.9, bf16[16,32,128]{2,1,0:T(8,128)(2,1)S(1)} %all_to_all.21.got, bf16[1024,1024]{1,0:T(8,128)(2,1)S(1)} %copy-done, f32[8,128]{1,0:T(8,128)S(1)} %bitcast.7, f32[8,128]{1,0:T(8,128)S(1)} %bitcast.8), custom_call_target="tpu_custom_call" | custom-call | flops 4000000000 | bytes 4000000 | tf_op jit(solution)/shard_map/pallas_call | solution.py:214
  42.8 9.8 %all_to_all.22.got = bf16[16,32,128]{2,1,0:T(8,128)(2,1)S(1)} all-to-all(bf16[16,32,128]{2,1,0:T(8,128)(2,1)S(1)} %shard_map.147), channel_id=1, replica_groups={{192,224,128,160,64,96,0,32,448,480,384,416,320,352,256,288},{193,225,1..., dimensions={0} | all-to-all | bytes 262144 | tf_op jit(solution)/shard_map/all_to_all | solution.py:228
  52.6 0.0 copy-start.2
  52.6 0.8 %shard_map.148 = bf16[32,16,128]{2,1,0:T(8,128)(2,1)S(1)} custom-call(bf16[16,32,128]{2,1,0:T(8,128)(2,1)S(1)} %all_to_all.22.got, bf16[1024,1024]{1,0:T(8,128)(2,1)S(1)} %copy-done.1), custom_call_target="tpu_custom_call" | custom-call | flops 4000000000 | bytes 4000000 | tf_op jit(solution)/shard_map/pallas_call | solution.py:214
  53.4 22.8 %all_to_all.23.got = bf16[32,16,128]{2,1,0:T(8,128)(2,1)S(1)} all-to-all(bf16[32,16,128]{2,1,0:T(8,128)(2,1)S(1)} %shard_map.148), channel_id=1, replica_groups={{21,20,23,22,17,16,19,18,29,28,31,30,25,24,27,26,5,4,7,6,1,0,3,2,13,12,..., dimensions={0} | all-to-all | bytes 262144 | tf_op jit(solution)/shard_map/all_to_all | solution.py:228
  76.3 0.0 copy-done.2
  76.3 1.3 %shard_map.149 = bf16[64,32,64]{2,1,0:T(8,128)(2,1)} custom-call(bf16[32,16,128]{2,1,0:T(8,128)(2,1)S(1)} %all_to_all.23.got, bf16[32,16,128]{2,1,0:T(8,128)(2,1)S(1)} %get-tuple-element.9.modal, f32[1024,128]{1,0:T(8,128)S(1)} %get-tuple-element.10.forcing, f32[32,64]{1,0:T(8,128)S(1)} %bitcast.6), custom_call_target="tpu_custom_call" | custom-call | flops 4000000000 | bytes 4000000 | tf_op jit(solution)/shard_map/pallas_call | solution.py:214
Async XLA Ops:
  0.0 29.5 %copy-start.1 = (bf16[1024,1024]{1,0:T(8,128)(2,1)S(1)}, bf16[1024,1024]{1,0:T(8,128)(2,1)}, u32[]{:S(2)}) copy-start(bf16[1024,1024]{1,0:T(8,128)(2,1)} %basis.5) | copy-start | bytes 6291460
  29.5 11.9 %copy-start = (bf16[1024,1024]{1,0:T(8,128)(2,1)S(1)}, bf16[1024,1024]{1,0:T(8,128)(2,1)}, u32[]{:S(2)}) copy-start(bf16[1024,1024]{1,0:T(8,128)(2,1)} %basis.4) | copy-start | bytes 6291460
  29.5 11.9 %copy-start.3 = (f32[1024]{0:T(1024)S(1)}, f32[1024]{0:T(1024)}, u32[]{:S(2)}) copy-start(f32[1024]{0:T(1024)} %param.27) | copy-start | bytes 12292
  29.5 11.9 %copy-start.4 = (f32[1024]{0:T(1024)S(1)}, f32[1024]{0:T(1024)}, u32[]{:S(2)}) copy-start(f32[1024]{0:T(1024)} %param.28) | copy-start | bytes 12292
  29.6 11.9 %copy-start.5 = (f32[32]{0:T(128)S(1)}, f32[32]{0:T(128)}, u32[]{:S(2)}) copy-start(f32[32]{0:T(128)} %param.29) | copy-start | bytes 388
  52.6 23.7 %copy-start.2 = (f32[64,32]{0,1:T(8,128)S(1)}, f32[64,32]{0,1:T(8,128)}, u32[]{:S(2)}) copy-start(f32[64,32]{0,1:T(8,128)} %param.22) | copy-start | bytes 24580

commit v5 on v4

--- a/solution.py
+++ b/solution.py
@@ -10,6 +10,7 @@
 HALF = 64
 LANES = 128
 GROUPS = 2
+OUT_GROUPS = 4
 MINUS_LOG2_E = -1.4426950408889634
 COL_MASK = 21
 ROW_MASK = 6
@@ -187,13 +188,16 @@
     difference[...] = gap.reshape(difference.shape)
     high, low = halves(restore[...])
     left = jnp.concatenate([high, low, high], axis=0)
-    for p in range(0, rows, 2):
-        correction = dot(left, right_terms(pair_of(difference, p, modes, rows)), 0, 0)
-        set_pair(total, p, correction, rows)
-    group = levels // GROUPS
+    right = [right_terms(pair_of(difference, p, modes, rows)) for p in range(0, rows, 2)]
+    group = levels // OUT_GROUPS
     copies = []
-    for k in range(GROUPS):
+    for k in range(OUT_GROUPS):
         cut = pl.ds(k * group, group)
+        for n in range(rows // 2):
+            correction = dot(left[:, k * group : (k + 1) * group], right[n], 0, 0)
+            for q in range(2):
+                here = pl.ds(k * group * rows + 2 * n + q, group, stride=rows)
+                total[here, :] = correction[:, q * LANES : (q + 1) * LANES]
         for level in range(k * group, (k + 1) * group):
             here = slice(level * rows, (level + 1) * rows)
             v = (forcing[here, :] + total[here, :]).astype(BF16)
@@ -307,7 +311,7 @@
             pltpu.VMEM(shape, BF16),
             pltpu.VMEM((modes * rows, LANES), F32),
             pltpu.VMEM((levels * rows, LANES), F32),
-            pltpu.SemaphoreType.DMA((GROUPS,)),
+            pltpu.SemaphoreType.DMA((OUT_GROUPS,)),
         ],
         exchange(send, "col"),
         modal,

time: 77.8 us -> 77.8 us (level)
  no operation moved by 1% of the time
where the time goes in v5:
time: 77.8 us; the launch traced here: 77.5 us
  blocking collectives  71 us (91%)
  Pallas kernels  6.5 us (8%)
    all_to_all x4, blocking collectives, exchange(): lax.all_to_all(v, axis, split_axis=0, concat_axis=0, tiled=True, axis_ind...  71 us
    pallas_call x5, Pallas kernels, call(): pl.pallas_call(body, in_specs=in_specs, out_specs=out_specs, out_shape=[j...  6.5 us

profile of v5, /device:TPU:1, one launch (start us, length us, event | category | flops | bytes accessed | tf_op | source)
XLA Modules:
  0.0 77.5 jit_solution(13887291532897996202)
XLA Ops:
  0.0 0.0 copy-start.1
  0.0 2.4 %shard_map.145 = (f32[1024,128]{1,0:T(8,128)S(1)}, bf16[32,16,128]{2,1,0:T(8,128)(2,1)S(1)}, bf16[32,16,128]{2,1,0:T(8,128)(2,1)S(1)}) custom-call(f32[4,64]{1,0:T(4,128)} %refs_0_.1, f32[4]{0:T(128)} %refs_1_.1, f32[4]{0:T(128)} %refs_2_.1, s32[16,32]{1,0:T(8,128)} %refs_3_.1, bf16[64,32,64]{2,1,0:T(8,128)(2,1)} %refs_4_.1, bf16[64,32,64]{2,1,0:T(8,128)(2,1)} %refs_5_.1, ...), custom_call_target="tpu_custom_call" | custom-call | flops 4000000000 | bytes 4000000 | tf_op jit(solution)/shard_map/pallas_call | solution.py:218
  2.4 27.2 %all_to_all.20.got = bf16[32,16,128]{2,1,0:T(8,128)(2,1)S(1)} all-to-all(bf16[32,16,128]{2,1,0:T(8,128)(2,1)S(1)} %get-tuple-element.8), channel_id=1, replica_groups={{21,20,23,22,17,16,19,18,29,28,31,30,25,24,27,26,5,4,7,6,1,0,3,2,13,12,..., dimensions={0} | all-to-all | bytes 262144 | tf_op jit(solution)/shard_map/all_to_all | solution.py:232
  29.5 0.0 copy-done.1
  29.5 0.0 copy-start
  29.5 0.0 copy-start.3
  29.5 0.0 copy-start.4
  29.6 0.0 copy-start.5
  29.6 0.7 shard_map.146
  30.3 11.2 %all_to_all.21.got = bf16[16,32,128]{2,1,0:T(8,128)(2,1)S(1)} all-to-all(bf16[16,32,128]{2,1,0:T(8,128)(2,1)S(1)} %shard_map.146), channel_id=1, replica_groups={{192,224,128,160,64,96,0,32,448,480,384,416,320,352,256,288},{193,225,1..., dimensions={0} | all-to-all | bytes 262144 | tf_op jit(solution)/shard_map/all_to_all | solution.py:232
  41.4 0.0 copy-done
  41.4 0.0 copy-done.3
  41.5 0.0 copy-done.4
  41.5 0.0 copy-done.5
  41.5 1.4 %shard_map.147 = bf16[16,32,128]{2,1,0:T(8,128)(2,1)S(1)} custom-call(f32[1,32]{1,0:T(1,128)S(1)} %bitcast.9, bf16[16,32,128]{2,1,0:T(8,128)(2,1)S(1)} %all_to_all.21.got, bf16[1024,1024]{1,0:T(8,128)(2,1)S(1)} %copy-done, f32[8,128]{1,0:T(8,128)S(1)} %bitcast.7, f32[8,128]{1,0:T(8,128)S(1)} %bitcast.8), custom_call_target="tpu_custom_call" | custom-call | flops 4000000000 | bytes 4000000 | tf_op jit(solution)/shard_map/pallas_call | solution.py:218
  42.8 9.8 %all_to_all.22.got = bf16[16,32,128]{2,1,0:T(8,128)(2,1)S(1)} all-to-all(bf16[16,32,128]{2,1,0:T(8,128)(2,1)S(1)} %shard_map.147), channel_id=1, replica_groups={{192,224,128,160,64,96,0,32,448,480,384,416,320,352,256,288},{193,225,1..., dimensions={0} | all-to-all | bytes 262144 | tf_op jit(solution)/shard_map/all_to_all | solution.py:232
  52.6 0.0 copy-start.2
  52.6 0.8 %shard_map.148 = bf16[32,16,128]{2,1,0:T(8,128)(2,1)S(1)} custom-call(bf16[16,32,128]{2,1,0:T(8,128)(2,1)S(1)} %all_to_all.22.got, bf16[1024,1024]{1,0:T(8,128)(2,1)S(1)} %copy-done.1), custom_call_target="tpu_custom_call" | custom-call | flops 4000000000 | bytes 4000000 | tf_op jit(solution)/shard_map/pallas_call | solution.py:218
  53.4 22.8 %all_to_all.23.got = bf16[32,16,128]{2,1,0:T(8,128)(2,1)S(1)} all-to-all(bf16[32,16,128]{2,1,0:T(8,128)(2,1)S(1)} %shard_map.148), channel_id=1, replica_groups={{21,20,23,22,17,16,19,18,29,28,31,30,25,24,27,26,5,4,7,6,1,0,3,2,13,12,..., dimensions={0} | all-to-all | bytes 262144 | tf_op jit(solution)/shard_map/all_to_all | solution.py:232
  76.3 0.0 copy-done.2
  76.3 1.2 %shard_map.149 = bf16[64,32,64]{2,1,0:T(8,128)(2,1)} custom-call(bf16[32,16,128]{2,1,0:T(8,128)(2,1)S(1)} %all_to_all.23.got, bf16[32,16,128]{2,1,0:T(8,128)(2,1)S(1)} %get-tuple-element.9.modal, f32[1024,128]{1,0:T(8,128)S(1)} %get-tuple-element.10.forcing, f32[32,64]{1,0:T(8,128)S(1)} %bitcast.6), custom_call_target="tpu_custom_call" | custom-call | flops 4000000000 | bytes 4000000 | tf_op jit(solution)/shard_map/pallas_call | solution.py:218
Async XLA Ops:
  0.0 29.5 %copy-start.1 = (bf16[1024,1024]{1,0:T(8,128)(2,1)S(1)}, bf16[1024,1024]{1,0:T(8,128)(2,1)}, u32[]{:S(2)}) copy-start(bf16[1024,1024]{1,0:T(8,128)(2,1)} %basis.5) | copy-start | bytes 6291460
  29.5 11.9 %copy-start = (bf16[1024,1024]{1,0:T(8,128)(2,1)S(1)}, bf16[1024,1024]{1,0:T(8,128)(2,1)}, u32[]{:S(2)}) copy-start(bf16[1024,1024]{1,0:T(8,128)(2,1)} %basis.4) | copy-start | bytes 6291460
  29.5 11.9 %copy-start.3 = (f32[1024]{0:T(1024)S(1)}, f32[1024]{0:T(1024)}, u32[]{:S(2)}) copy-start(f32[1024]{0:T(1024)} %param.27) | copy-start | bytes 12292
  29.5 11.9 %copy-start.4 = (f32[1024]{0:T(1024)S(1)}, f32[1024]{0:T(1024)}, u32[]{:S(2)}) copy-start(f32[1024]{0:T(1024)} %param.28) | copy-start | bytes 12292
  29.6 11.9 %copy-start.5 = (f32[32]{0:T(128)S(1)}, f32[32]{0:T(128)}, u32[]{:S(2)}) copy-start(f32[32]{0:T(128)} %param.29) | copy-start | bytes 388
  52.6 23.7 %copy-start.2 = (f32[64,32]{0,1:T(8,128)S(1)}, f32[64,32]{0,1:T(8,128)}, u32[]{:S(2)}) copy-start(f32[64,32]{0,1:T(8,128)} %param.22) | copy-start | bytes 24580
